TPU v7x, 32 devices: a whole 2x2x4 slice. The times are simulated.
32 devices in a mesh: seq: 8 (over y, x, core), kvh: 4 (over z).
Axes of the slice: x: 2, y: 2, z: 4, core: 2. Of those that a mesh axis runs over, the one named last changes fastest.
Arguments:
- queries: bfloat16 [64, 64, 128], P(None, 'kvh'), may hold values from -128 to 128
- keys: bfloat16 [1024, 8, 128, 128], P('seq', 'kvh'), may hold values from -6 to 6
- values: bfloat16 [1024, 8, 128, 128], P('seq', 'kvh'), may hold values from -6 to 6
- rep_keys: bfloat16 [1024, 8, 4, 128], P('seq', 'kvh'), may hold values from -8 to 8
- rep_values: bfloat16 [1024, 8, 4, 128], P('seq', 'kvh'), may hold values from -6 to 6
- block_ids: int32 [64, 8, 16], P(None, 'kvh'), may hold values from 0 to 1023, as said below
- block_counts: int32 [1024], P('seq'), may hold values from 64 to 128
- out_weight: bfloat16 [8192, 8192], P('kvh', 'seq'), may hold values from -0.5 to 0.5
Outputs:
- projected: bfloat16 [64, 8192], P('kvh', 'seq')
Inputs may be any that keep to these rules, and one draw needn't show every extreme that they name: `block_ids`: for every token and key-value head the 16 ids are different. For every key-value head at most 192 of its 64 x 16 ids lie among the blocks o * 128 to (o + 1) * 128 - 1 of one o, and for some o exactly 192.
All inputs are finite; a program needn't handle non-finite values.
Results may differ from a plain program's by a relative error of at most 0.023.
Values may be sent and summed in bfloat16 or wider, within the bound.
A program may use at most 128 MiB of HBM per device.

v0:
```python
import math

import jax
import jax.numpy as jnp
from jax import lax
from jax.sharding import PartitionSpec as P

FLOOR_SCORE = -1e30


def joined(value, axis, combine):
    everything = jax.tree.map(
        lambda part, kind: lax.all_gather(part.astype(kind), axis),
        value,
        jax.tree.map(lambda a: jnp.bfloat16 if a.dtype == jnp.float32 else a.dtype, value),
    )

    def take(k):
        return jax.tree.map(lambda part, own: part[k].astype(own.dtype), everything, value)

    return lax.fori_loop(
        1, lax.axis_size(axis), lambda k, so_far: combine(so_far, take(k)), take(0)
    )


def combine(former, latter):
    highest = jnp.maximum(former[0], latter[0])
    first_factor = jnp.exp(former[0] - highest)
    second_factor = jnp.exp(latter[0] - highest)
    weight_sum = former[1] * first_factor + latter[1] * second_factor
    weighted = former[2] * first_factor[..., None] + latter[2] * second_factor[..., None]
    return (highest, weight_sum, weighted)


def summary_stats(query_rows, summary_keys, summary_vals):
    inv_root = 1.0 / math.sqrt(query_rows.shape[-1])
    scores = (
        jnp.einsum("bkgd,nkrd->bkgrn", query_rows, summary_keys, preferred_element_type=jnp.float32)
        * inv_root
    )
    highest = jnp.max(scores, axis=(3, 4))
    weights = jnp.exp(scores - highest[..., None, None])
    weight_sum = jnp.sum(weights, axis=(3, 4))
    weighted = jnp.einsum(
        "bkgrn,nkrd->bkgd",
        weights.astype(jnp.bfloat16),
        summary_vals,
        preferred_element_type=jnp.float32,
    )
    return (highest, weight_sum, weighted)


def chosen_stats(query_rows, tile_keys, tile_vals, slot_token, slot_count, slot_live):
    num_tokens = query_rows.shape[0]
    block_width = tile_keys.shape[2]
    inv_root = 1.0 / math.sqrt(query_rows.shape[-1])
    heads_here = jnp.arange(tile_keys.shape[0], dtype=jnp.int32)
    slot_query = query_rows[slot_token, heads_here[:, None]]
    scores = (
        jnp.einsum("kjgd,kjtd->kjgt", slot_query, tile_keys, preferred_element_type=jnp.float32)
        * inv_root
    )
    inside = jnp.arange(block_width, dtype=jnp.int32)[None, None, :] < slot_count[:, :, None]
    allowed = (inside & slot_live[:, :, None])[:, :, None, :]
    scores = jnp.where(allowed, scores, FLOOR_SCORE)
    slot_max = jnp.max(scores, axis=3)
    owner_map = slot_token[None, :, :] == jnp.arange(num_tokens, dtype=jnp.int32)[:, None, None]
    highest = jnp.max(jnp.where(owner_map[..., None], slot_max[None], FLOOR_SCORE), axis=2)
    slot_high = highest[slot_token, heads_here[:, None]]
    weights = jnp.where(allowed, jnp.exp(scores - slot_high[..., None]), 0.0)
    token_onehot = owner_map.astype(jnp.float32)
    weight_sum = jnp.einsum(
        "bkj,kjg->bkg", token_onehot, jnp.sum(weights, axis=3), precision=lax.Precision.HIGHEST
    )
    slot_weighted = jnp.einsum(
        "kjgt,kjtd->kjgd",
        weights.astype(jnp.bfloat16),
        tile_vals,
        preferred_element_type=jnp.float32,
    )
    weighted = jnp.einsum(
        "bkj,kjgd->bkgd", token_onehot, slot_weighted, precision=lax.Precision.HIGHEST
    )
    return (highest, weight_sum, weighted)


def on_device(queries, keys, values, rep_keys, rep_values, block_ids, block_counts, out_weight):
    num_tokens = queries.shape[0]
    local_heads = keys.shape[1]
    blocks_here = keys.shape[0]
    chosen_count = block_ids.shape[2]
    query_rows = queries.reshape(num_tokens, local_heads, -1, queries.shape[2])
    seq_index = lax.axis_index("seq")
    flat_ids = jnp.transpose(block_ids, (1, 0, 2)).reshape(local_heads, num_tokens * chosen_count)
    pair_token = jnp.arange(num_tokens * chosen_count, dtype=jnp.int32) // chosen_count
    head_pos = jnp.arange(local_heads, dtype=jnp.int32)
    capacity = 3 * num_tokens
    local_pair = flat_ids // blocks_here == seq_index
    local_rank = jnp.cumsum(local_pair.astype(jnp.int32), axis=1) - 1
    slot_ids = jnp.arange(capacity, dtype=jnp.int32)
    chosen_map = local_pair[:, None, :] & (local_rank[:, None, :] == slot_ids[None, :, None])
    slot_live = jnp.any(chosen_map, axis=2)
    slot_block = jnp.sum(jnp.where(chosen_map, flat_ids[:, None, :] % blocks_here, 0), axis=2)
    slot_token = jnp.sum(jnp.where(chosen_map, pair_token[None, None, :], 0), axis=2)
    tile_keys = keys[slot_block, head_pos[:, None]]
    tile_vals = values[slot_block, head_pos[:, None]]
    slot_count = block_counts[slot_block]
    chosen = chosen_stats(query_rows, tile_keys, tile_vals, slot_token, slot_count, slot_live)
    stat_shape = query_rows.shape[:3]
    initial = (
        jnp.full(stat_shape, FLOOR_SCORE, jnp.float32),
        jnp.zeros(stat_shape, jnp.float32),
        jnp.zeros(query_rows.shape, jnp.float32),
    )
    summary = combine(
        initial,
        summary_stats(
            query_rows,
            lax.all_gather(rep_keys, "seq", axis=0, tiled=True),
            lax.all_gather(rep_values, "seq", axis=0, tiled=True),
        ),
    )
    merged = joined(chosen, "seq", combine)
    merged = combine(merged, summary)
    attended = (merged[2] / merged[1][..., None]).astype(jnp.bfloat16).reshape(num_tokens, -1)
    terms = jnp.dot(attended, out_weight, preferred_element_type=jnp.float32)
    return lax.psum_scatter(terms.astype(jnp.bfloat16), "kvh", scatter_dimension=0, tiled=True)


def solution(mesh):
    in_specs = (
        P(None, "kvh", None),
        P("seq", "kvh", None, None),
        P("seq", "kvh", None, None),
        P("seq", "kvh", None, None),
        P("seq", "kvh", None, None),
        P(None, "kvh", None),
        P("seq"),
        P("kvh", "seq"),
    )
    out_specs = P("kvh", "seq")
    return jax.shard_map(
        on_device, mesh=mesh, in_specs=in_specs, out_specs=out_specs, check_vma=False
    )
```

profile of v0, /device:TPU:0, one launch (start us, length us, event | category | flops | bytes accessed | tf_op | source)
XLA Modules:
  0.0 204.2 jit_solution(15480267772740739778)
XLA Ops:
  6.5 0.8 copy.91
  7.7 0.6 reduce-window.6
  8.2 0.2 slice_reduce_fusion
  8.5 0.2 reduce-window.9
  8.7 0.3 fusion.14
  9.0 0.7 select_reduce_fusion
  9.9 3.4 %gather_fusion = s32[384]{0:T(512)S(1)} fusion(s32[128]{0:T(128)} %param.16, s32[1024]{0:T(1024)S(1)} %pad_clamp_fusion), kind=kCustom, calls=%fused_computation | custom fusion | bytes 4608 | tf_op jit(solution)/shard_map/gather | solution.py:107
  13.6 0.2 fusion.67
  13.8 19.8 %gather_fusion.2 = bf16[384,128,128]{2,1,0:T(8,128)(2,1)} fusion(bf16[128,2,128,128]{3,2,1,0:T(8,128)(2,1)} %param.11, s32[384]{0:T(512)S(1)} %reshape.210), kind=kCustom, calls=%fused_computation.2 | custom fusion | bytes 25168896 | tf_op jit(solution)/shard_map/gather | solution.py:105
  33.6 2.0 gather_fusion.1
  35.6 9.3 %fusion.92 = (f32[2,192,8]{2,1,0:T(8,128)S(1)}, f32[2,192,8,128]{3,2,1,0:T(8,128)S(1)}) fusion(bf16[2,192,8,128]{3,2,1,0:T(8,128)(2,1)S(1)} %bitcast.141, bf16[2,192,128,128]{3,2,1,0:T(8,128)(2,1)} %bitcast.139, pred[2,192,128]{2,1,0:T(8,128)(4,1)S(1)} %fusion.67), kind=kOutput, calls=%fused_computation.112 | convolution fusion | flops 101839872 | bytes 15003648 | tf_op jit(solution)/shard_map/kjgd,kjtd->kjgt/dot_general | solution.py:60
  44.8 0.1 copy.94
  45.0 0.3 select_reduce_fusion.2
  45.3 2.4 %gather_fusion.3 = f32[384,8]{1,0:T(8,128)S(1)} fusion(f32[64,2,8]{2,1,0:T(2,128)S(1)} %select_reduce_fusion.2, s32[384]{0:T(512)S(1)} %reshape.204), kind=kCustom, calls=%fused_computation.3 | custom fusion | bytes 27648 | tf_op jit(solution)/shard_map/gather | solution.py:69
  47.8 19.8 %gather_fusion.4 = bf16[384,128,128]{2,1,0:T(8,128)(2,1)} fusion(bf16[128,2,128,128]{3,2,1,0:T(8,128)(2,1)} %param.12, s32[384]{0:T(512)S(1)} %reshape.210), kind=kCustom, calls=%fused_computation.4 | custom fusion | bytes 25168896 | tf_op jit(solution)/shard_map/gather | solution.py:106
  67.6 6.9 %fusion.59 = f32[2,192,8,128]{3,2,1,0:T(8,128)S(1)} fusion(bf16[2,192,128,128]{3,2,1,0:T(8,128)(2,1)} %bitcast.140, f32[2,192,8,128]{3,2,1,0:T(8,128)S(1)} %get-tuple-element.254, f32[2,192,8]{2,1,0:T(8,128)S(1)} %bitcast.142, pred[2,192,128]{2,1,0:T(8,128)(4,1)S(1)} %fusion.67), kind=kOutput, calls=%fused_computation.48 | convolution fusion | flops 101842944 | bytes 15790080 | tf_op jit(solution)/shard_map/kjgt,kjtd->kjgd/dot_general | solution.py:75
  74.5 1.6 fusion.45
  76.1 0.7 copy.104
  76.9 0.7 copy.107
  77.8 1.0 fusion.16
  78.8 0.3 fusion.58
  79.0 0.1 copy.96
  79.2 10.9 %all-gather.1 = bf16[512,2,8]{2,1,0:T(2,128)(2,1)S(1)} all-gather(bf16[64,2,8]{2,1,0:T(2,128)(2,1)S(1)} %copy.96), channel_id=3, replica_groups=mesh['seq'=8,'kvh'=4] {'seq'}, dimensions={0}, use_global_device_ids=true | all-gather | bytes 18432 | tf_op jit(solution)/shard_map/all_gather | solution.py:13
  90.2 0.1 copy.102
  90.3 9.7 %all-gather = bf16[512,2,8]{2,1,0:T(2,128)(2,1)S(1)} all-gather(bf16[64,2,8]{2,1,0:T(2,128)(2,1)S(1)} %convert_element_type.100), channel_id=2, replica_groups=mesh['seq'=8,'kvh'=4] {'seq'}, dimensions={0}, use_global_device_ids=true | all-gather | bytes 18432 | tf_op jit(solution)/shard_map/all_gather | solution.py:13
  100.1 0.1 copy.101
  100.3 6.7 %all-gather.11.cloned.1.call-done = bf16[512,2,8,128]{3,0,2,1:T(8,128)(2,1)} async-done(((bf16[64,2,8,128]{3,0,2,1:T(8,128)(2,1)}), bf16[512,2,8,128]{3,0,2,1:T(8,128)(2,1)}) %all-gather.11.cloned.1.call-update) | async-done | bytes 2097168 | tf_op jit(solution)/shard_map/all_gather | solution.py:13
  107.0 1.0 slice_convert_fusion
  108.0 0.3 copy.100
  108.3 28.4 %all-gather.7.cloned.1.call-done = bf16[1024,2,4,128]{3,0,2,1:T(8,128)(2,1)} async-done(((bf16[128,2,4,128]{3,0,2,1:T(8,128)(2,1)}), bf16[1024,2,4,128]{3,0,2,1:T(8,128)(2,1)}) %all-gather.7.cloned.1.call-update) | async-done | bytes 2097168 | tf_op jit(solution)/shard_map/all_gather | solution.py:119
  136.7 9.8 %bitcast_reduce_fusion = (f32[64,2,8]{0,2,1:T(8,128)S(1)}, f32[2,1024,4,64,8]{1,3,4,2,0:T(8,128)}) fusion(bf16[64,2,8,128,1]{3,2,1,0,4:T(8,128)(2,1)S(1)} %bitcast.138, bf16[1024,2,4,128]{3,0,2,1:T(8,128)(2,1)} %all-gather.7.cloned.1.call-done), kind=kOutput, calls=%fused_computation.16 | convolution fusion | flops 1082129408 | bytes 19140608 | tf_op jit(solution)/shard_map/bkgd,nkrd->bkgrn/dot_general | solution.py:38
  146.5 8.6 %fusion.4 = f32[64,2,8]{0,2,1:T(8,128)S(1)} fusion(f32[2,1024,4,64,8]{1,3,4,2,0:T(8,128)} %get-tuple-element.252, f32[64,2,8]{0,2,1:T(8,128)S(1)} %get-tuple-element.251), kind=kLoop, calls=%fused_computation.18 | loop fusion | flops 12581888 | bytes 16785408 | tf_op jit(solution)/shard_map/reduce_sum | solution.py:43
  155.1 12.7 %while.19 = (s32[]{:T(128)}, f32[64,2,8]{0,2,1:T(8,128)S(1)}, f32[64,2,8]{0,2,1:T(8,128)S(1)}, f32[64,2,8,128]{3,2,1,0:T(8,128)S(1)}, bf16[8,64,2,8]{1,3,2,0:T(8...) while((s32[]{:T(128)}, f32[64,2,8]{0,2,1:T(8,128)S(1)}, ...), condition=%wide.region_9.10_spmd, body=%wide.region_8.9_spmd.sunk | while | flops 532485 | bytes 1888407 | solution.py:21
  155.3 0.1 copy.147
  155.4 0.1 copy.148
  155.5 1.0 constant_dynamic-slice_fusion.2
  156.5 0.5 fusion.101
  157.1 0.1 copy.147
  157.2 0.1 copy.148
  157.3 1.0 constant_dynamic-slice_fusion.2
  158.3 0.5 fusion.101
  158.9 0.1 copy.147
  159.0 0.1 copy.148
  159.1 1.0 constant_dynamic-slice_fusion.2
  160.1 0.5 fusion.101
  160.7 0.1 copy.147
  160.8 0.1 copy.148
  160.9 1.0 constant_dynamic-slice_fusion.2
  161.9 0.5 fusion.101
  162.5 0.1 copy.147
  162.6 0.1 copy.148
  162.7 1.0 constant_dynamic-slice_fusion.2
  163.7 0.5 fusion.101
  164.3 0.1 copy.147
  164.4 0.1 copy.148
  164.5 1.0 constant_dynamic-slice_fusion.2
  165.5 0.5 fusion.101
  166.2 0.1 copy.148
  166.3 1.0 constant_dynamic-slice_fusion.2
  167.3 0.5 fusion.101
  167.9 8.4 %fusion.53 = bf16[64,2,8,128]{3,0,2,1:T(8,128)(2,1)S(1)} fusion(bf16[1024,2,4,128]{3,0,2,1:T(8,128)(2,1)} %all-gather.9.cloned.1.call-done, f32[2,1024,4,64,8]{1,3,4,2,0:T(8,128)} %get-tuple-element.252, f32[64,2,8]{0,2,1:T(8,128)S(1)} %get-tuple-element.251, f32[64,2,8,128]{3,2,1,0:T(8,128)S(1)} %get-tuple-element.183, ...), kind=kOutput, calls=%fused_computation.44 | convolution fusion | flops 1087242240 | bytes 19685376 | tf_op jit(solution)/shard_map/bkgrn,nkrd->bkgd/dot_general | solution.py:44
  176.3 0.2 copy.109
  176.5 1.5 convolution_convert_fusion
  178.0 19.7 %reduce-scatter.2.cloned.1.call-done = bf16[16,1024]{1,0:T(8,128)(2,1)} async-done(((bf16[64,1024]{1,0:T(8,128)(2,1)}), bf16[16,1024]{1,0:T(8,128)(2,1)}) %reduce-scatter.2.cloned.1.call-update) | async-done | bytes 32784 | tf_op jit(solution)/shard_map/reduce_scatter | solution.py:127
  (49 shorter events, 1.5 us)
Async XLA Ops:
  6.5 27.0 %copy-start = (bf16[64,16,128]{2,1,0:T(8,128)(2,1)S(1)}, bf16[64,16,128]{2,1,0:T(8,128)(2,1)}, u32[]{:S(2)}) copy-start(bf16[64,16,128]{2,1,0:T(8,128)(2,1)} %param.10) | copy-start | bytes 786436
  6.5 100.5 %all-gather.11.cloned.1.call-start = ((), (), s32[]{:S(2)}) async-start(), calls=%async_computation.4 | async-start | bytes 2359296 | tf_op jit(solution)/shard_map/all_gather | solution.py:13
  74.5 1.6 copy-start.3
  74.5 2.5 %copy-start.4 = (bf16[128,2,4,128]{3,2,1,0:T(4,128)(2,1)S(1)}, bf16[128,2,4,128]{3,2,1,0:T(4,128)(2,1)}, u32[]{:S(2)}) copy-start(bf16[128,2,4,128]{3,2,1,0:T(4,128)(2,1)} %param.14) | copy-start | bytes 786436
  76.1 60.6 %all-gather.7.cloned.1.call-start = ((), (), s32[]{:S(2)}) async-start(), calls=%async_computation.1 | async-start | bytes 2359296 | tf_op jit(solution)/shard_map/all_gather | solution.py:119
  76.9 91.0 %all-gather.9.cloned.1.call-start = ((), (), s32[]{:S(2)}) async-start(), calls=%async_computation.2 | async-start | bytes 2359296 | tf_op jit(solution)/shard_map/all_gather | solution.py:120
  77.7 120.0 %reduce-scatter.2.cloned.1.call-start = ((), (), s32[]{:S(2)}) async-start(), calls=%async_computation.3 | async-start | bytes 163840 | tf_op jit(solution)/shard_map/reduce_scatter | solution.py:127
  167.9 8.6 %copy-start.2 = (bf16[2048,1024]{1,0:T(8,128)(2,1)S(1)}, bf16[2048,1024]{1,0:T(8,128)(2,1)}, u32[]{:S(2)}) copy-start(bf16[2048,1024]{1,0:T(8,128)(2,1)} %param.17) | copy-start | bytes 12582916
  176.5 21.2 %copy-start.1 = (bf16[64,16,128]{2,1,0:T(8,128)(2,1)S(1)}, bf16[64,16,128]{2,1,0:T(8,128)(2,1)}, u32[]{:S(2)}) copy-start(bf16[64,16,128]{2,1,0:T(8,128)(2,1)} %param.10) | copy-start | bytes 786436
Sparse Core Ops, SparseCore 0:
  76.2 30.7 all-gather.10
  108.9 27.7 all-gather.6
  138.6 27.7 all-gather.8
  178.2 19.4 reduce-scatter.1
where the time goes:
time: 205 us; the launch traced here: 204 us
  local copies, waits for them, and re-layouts  60 us (29%)
  waiting for transfers between devices  54.9 us (27%)
  matrix products  37.7 us (18%)
  blocking collectives  20.6 us (10%)
  other arithmetic  17 us (8%)
  between operations  13.4 us (7%)
    all_gather x1, waiting for transfers between devices, on_device(): lax.all_gather(rep_keys, 'seq', axis=0, tiled=True)  28.4 us
    all_gather x2, blocking collectives, joined(): lax.all_gather(part.astype(kind), axis)  20.6 us
    gather x1, local copies, waits for them, and re-layouts, on_device(): tile_vals = values[slot_block, head_pos[:, None]]  19.8 us
    gather x1, local copies, waits for them, and re-layouts, on_device(): tile_keys = keys[slot_block, head_pos[:, None]]  19.8 us
    reduce_scatter x1, waiting for transfers between devices, on_device(): lax.psum_scatter(terms.astype(jnp.bfloat16), 'kvh', scatter_dimension=0,...  19.7 us
    dot_general x1, matrix products, summary_stats(): jnp.einsum('bkgd,nkrd->bkgrn', query_rows, summary_keys, preferred_elemen...  9.76 us
    dot_general x1, matrix products, chosen_stats(): jnp.einsum('kjgd,kjtd->kjgt', slot_query, tile_keys, preferred_element_ty...  9.27 us
    reduce_sum x1, other arithmetic, summary_stats(): weight_sum = jnp.sum(weights, axis=(3, 4))  8.64 us
  transfers between devices with their start and end apart: 4, of which 3 were waited for; matrix products, arithmetic and copies ran while one was open for 17% of the time, Pallas kernels for 0%

commit v1 on v0

v1 whole, which is shorter than its diff:
```python
import functools
import math

import jax
import jax.numpy as jnp
from jax import lax
from jax.experimental import pallas as pl
from jax.experimental.pallas import tpu as pltpu
from jax.sharding import PartitionSpec as P

FLOOR_SCORE = -1e30
LANES = 128
UNROLL = 16
PIECES = 4
MESH = pl.DeviceIdType.MESH


def contract_last(a, b):
    return lax.dot_general(a, b, (((1,), (1,)), ((), ())), preferred_element_type=jnp.float32)


def matmul(a, b):
    return jnp.dot(a, b, preferred_element_type=jnp.float32)


def attend_kernel(
    counts_ref, ids_ref, q_ref, rk_ref, rv_ref, keys_ref, values_ref, o_ref, lse_ref,
    k_mem, v_mem, slots_v, slots_s, qh, sums, sc, top, low, acc, k_sem, v_sem, slot_sem,
):
    tokens, heads, width = q_ref.shape
    kv_heads, blocks, span, _ = k_mem.shape
    group = heads // kv_heads
    reps = rk_ref.shape[1]
    chosen = ids_ref.shape[2]
    lanes = slots_v.shape[1]
    inv_root = 1.0 / math.sqrt(width)
    me = lax.axis_index("seq")

    part = blocks // PIECES

    def copy_of(k, i, source, target, sem):
        rows = pl.ds(i * part, part)
        return pltpu.make_async_copy(source.at[rows, k], target.at[k, rows], sem.at[k, i])

    for k in range(kv_heads):
        for i in range(PIECES):
            copy_of(k, i, keys_ref, k_mem, k_sem).start()
        for i in range(PIECES):
            copy_of(k, i, values_ref, v_mem, v_sem).start()

    token_of = lax.broadcasted_iota(jnp.int32, (tokens, chosen), 0)
    slot_of = lax.broadcasted_iota(jnp.int32, (tokens, lanes), 1)
    before_slot = (
        lax.broadcasted_iota(jnp.int32, (chosen, chosen), 0)
        < lax.broadcasted_iota(jnp.int32, (chosen, chosen), 1)
    ).astype(jnp.bfloat16)
    before_token = (
        lax.broadcasted_iota(jnp.int32, (tokens, tokens), 1)
        < lax.broadcasted_iota(jnp.int32, (tokens, tokens), 0)
    ).astype(jnp.bfloat16)
    every_slot = jnp.ones((chosen, chosen), jnp.bfloat16)
    slots_v[...] = jnp.zeros_like(slots_v)
    for k in range(kv_heads):
        ids = ids_ref[:, k, :] - me * blocks
        here = (ids >= 0) & (ids < blocks)
        mark = jnp.where(here, 1.0, 0.0).astype(jnp.bfloat16)
        of_token = matmul(mark, every_slot)
        rank = matmul(mark, before_slot) + matmul(before_token, of_token.astype(jnp.bfloat16))
        rank = jnp.where(here, rank.astype(jnp.int32), -1)
        code = token_of * blocks + ids + 1
        found = jnp.zeros((tokens, lanes), jnp.int32)
        for s in range(chosen):
            found = found + jnp.where(rank[:, s : s + 1] == slot_of, code[:, s : s + 1], 0)
        slots_v[k : k + 1, :] = jnp.sum(found, axis=0, keepdims=True)
        total = jnp.sum(of_token[:, 0:1], axis=0, keepdims=True).astype(jnp.int32)
        slots_v[kv_heads + k : kv_heads + k + 1, :] = jnp.broadcast_to(total, (1, lanes))
    slot_copy = pltpu.make_async_copy(slots_v, slots_s, slot_sem)
    slot_copy.start()

    for k in range(kv_heads):
        mine = q_ref[...].astype(jnp.float32)[:, k * group : (k + 1) * group, :]
        qh[k] = mine.reshape(tokens * group, width).astype(jnp.bfloat16)
        scores = contract_last(qh[k], rk_ref[k]) * inv_root
        sums[k] = scores
        most = scores[:, :LANES]
        for c in range(LANES, reps, LANES):
            most = jnp.maximum(most, scores[:, c : c + LANES])
        top[k] = most.reshape(tokens, group, LANES)

    slot_copy.wait()
    lane = lax.broadcasted_iota(jnp.int32, (group, span), 1)

    def slot(k, j):
        code = slots_s[k, j]
        at = jnp.maximum(code - 1, 0)
        token = lax.div(at, blocks)
        return code, token, at - token * blocks

    for k in range(kv_heads):
        rounds = lax.div(slots_s[kv_heads + k, 0] + (UNROLL - 1), UNROLL)

        for i in range(PIECES):
            copy_of(k, i, keys_ref, k_mem, k_sem).wait()

        def score_round(i, carry, k=k):
            places, found = [], []
            for u in range(UNROLL):
                j = i * UNROLL + u
                code, token, block = slot(k, j)
                count = jnp.where(code > 0, counts_ref[block], 0)
                s = contract_last(q_ref[token], k_mem[k, block])
                s = s[k * group : (k + 1) * group] * inv_root
                s = jnp.where(lane < count, s, FLOOR_SCORE)
                sc[j] = s
                places.append(token)
                found.append(s)
            for token, s in zip(places, found):
                top[k, token] = jnp.maximum(top[k, token], s)
            return carry

        lax.fori_loop(0, rounds, score_round, 0)

        most = jnp.max(top[k], axis=2, keepdims=True)
        top[k] = jnp.broadcast_to(most, (tokens, group, LANES))
        weights = jnp.exp(sums[k] - most.reshape(tokens * group, 1))
        some = weights[:, :LANES]
        for c in range(LANES, reps, LANES):
            some = some + weights[:, c : c + LANES]
        low[k] = some.reshape(tokens, group, LANES)
        acc[k] = matmul(weights.astype(jnp.bfloat16), rv_ref[k]).reshape(tokens, group, width)

        for i in range(PIECES):
            copy_of(k, i, values_ref, v_mem, v_sem).wait()

        def weight_round(i, carry, k=k):
            places, found, parts = [], [], []
            for u in range(UNROLL):
                j = i * UNROLL + u
                _, token, block = slot(k, j)
                p = jnp.exp(sc[j] - top[k, token])
                places.append(token)
                found.append(p)
                parts.append(matmul(p.astype(jnp.bfloat16), v_mem[k, block]))
            for token, p, o in zip(places, found, parts):
                low[k, token] = low[k, token] + p
                acc[k, token] = acc[k, token] + o
            return carry

        lax.fori_loop(0, rounds, weight_round, 0)

        weight_sum = jnp.sum(low[k], axis=2, keepdims=True)
        low[k] = top[k] + jnp.log(jnp.broadcast_to(weight_sum, (tokens, group, LANES)))
        acc[k] = acc[k] / weight_sum

    shares, rows, _ = o_ref.shape
    run = min(rows, tokens)
    diagonal = lax.broadcasted_iota(jnp.int32, (run, LANES), 0)
    column = lax.broadcasted_iota(jnp.int32, (run, LANES), 1)
    for share in range(shares):
        line = jnp.zeros((1, LANES), jnp.float32)
        for at in range(0, rows, run):
            head, token = divmod(share * rows + at, tokens)
            k, g = divmod(head, group)
            o_ref[share, at : at + run, :] = acc[k, token : token + run, g, :].astype(jnp.bfloat16)
            lse = low[k, token : token + run, g, :]
            line += jnp.sum(
                jnp.where(diagonal + at == column, lse, 0.0), axis=0, keepdims=True
            )
        lse_ref[share] = jnp.broadcast_to(line, lse_ref.shape[1:])


def finish_kernel(
    shares, groups, o_ref, lse_ref, w_ref, out_ref,
    w_mem, o_in, lse_in, attended, total, part_out, part_in,
    w_sem, o_send, o_recv, lse_send, lse_recv, a_send, a_recv, p_send, p_recv,
):
    me, mine = lax.axis_index("seq"), lax.axis_index("kvh")
    _, rows, width = o_ref.shape
    tokens, columns = total.shape

    def w_copy(i):
        depth = w_ref.shape[0] // shares
        return pltpu.make_async_copy(
            w_ref.at[pl.ds(i * depth, depth)], w_mem.at[pl.ds(i * depth, depth)], w_sem.at[i]
        )

    for i in range(shares):
        w_copy(i).start()

    barrier = pltpu.get_barrier_semaphore()
    for d in range(1, shares):
        pl.semaphore_signal(
            barrier, inc=1, device_id={"seq": lax.rem(me + d, shares)}, device_id_type=MESH
        )
    for d in range(1, groups):
        pl.semaphore_signal(
            barrier, inc=1, device_id={"kvh": lax.rem(mine + d, groups)}, device_id_type=MESH
        )
    pl.semaphore_wait(barrier, shares - 1 + groups - 1)

    def send(source, target, sent, got, axis, peer):
        copy = pltpu.make_async_remote_copy(
            src_ref=source, dst_ref=target, send_sem=sent, recv_sem=got,
            device_id={axis: peer}, device_id_type=MESH,
        )
        copy.start()
        return copy

    spread = []
    for d in range(1, shares):
        peer = lax.rem(me + d, shares)
        spread.append(send(
            lse_ref.at[peer], lse_in.at[me], lse_send.at[d], lse_recv.at[d], "seq", peer))
        spread.append(send(o_ref.at[peer], o_in.at[me], o_send.at[d], o_recv.at[d], "seq", peer))
    lse_in[me] = lse_ref[me]
    o_in[me] = o_ref[me]
    for copy in spread:
        copy.wait_recv()

    lse = [lse_in[i][0:1] for i in range(shares)]
    highest = functools.reduce(jnp.maximum, lse)
    factors = [jnp.exp(one - highest) for one in lse]
    inverse = 1.0 / functools.reduce(jnp.add, factors)
    on_diagonal = lax.broadcasted_iota(jnp.int32, (rows, LANES), 0) == lax.broadcasted_iota(
        jnp.int32, (rows, LANES), 1
    )
    joined = jnp.zeros((rows, width), jnp.float32)
    for i in range(shares):
        factor = jnp.where(on_diagonal, factors[i] * inverse, 0.0)
        joined += jnp.sum(factor, axis=1, keepdims=True) * o_in[i].astype(jnp.float32)
    attended[me] = joined.astype(jnp.bfloat16)

    gathered = []
    for d in range(1, shares):
        peer = lax.rem(me + d, shares)
        gathered.append(send(
            attended.at[me], attended.at[me], a_send.at[d], a_recv.at[d], "seq", peer))

    for i in range(shares):
        w_copy(i).wait()
    if rows % tokens == 0:
        depth = rows // tokens * width
        for d in range(shares):
            if d:
                gathered[d - 1].wait_recv()
            owner = lax.rem(me - d + shares, shares)
            block = attended[owner]
            left = jnp.concatenate(
                [block[at : at + tokens] for at in range(0, rows, tokens)], axis=1
            )
            right = w_mem[pl.ds(pl.multiple_of(owner * depth, depth), depth), :]
            term = matmul(left, right)
            total[...] = term if d == 0 else total[...] + term
    else:
        for copy in gathered:
            copy.wait_recv()
        pieces = tokens // rows
        for head in range(shares // pieces):
            left = jnp.concatenate([attended[head * pieces + p] for p in range(pieces)], axis=0)
            term = matmul(left, w_mem[head * width : (head + 1) * width, :])
            total[...] = term if head == 0 else total[...] + term

    here = tokens // groups
    part_out[...] = total[...].astype(jnp.bfloat16).reshape(part_out.shape)
    parts = []
    for d in range(1, groups):
        peer = lax.rem(mine + d, groups)
        parts.append(send(
            part_out.at[peer], part_in.at[mine], p_send.at[d], p_recv.at[d], "kvh", peer))
    result = total[pl.ds(pl.multiple_of(mine * here, here), here), :]
    for d in range(1, groups):
        parts[d - 1].wait_recv()
        result = result + part_in[lax.rem(mine - d + groups, groups)].astype(jnp.float32)
    out_ref[...] = result.astype(out_ref.dtype)
    for copy in spread + gathered + parts:
        copy.wait_send()


def on_device(
    shares, groups, queries, keys, values, rep_keys, rep_values, block_ids, block_counts, out_weight
):
    tokens, heads, width = queries.shape
    blocks, kv_heads, span, _ = keys.shape
    group = heads // kv_heads
    reps = blocks * rep_keys.shape[2]
    rows = heads * tokens // shares
    columns = out_weight.shape[1]
    capacity = -(-3 * tokens // UNROLL) * UNROLL
    lanes = -(-capacity // LANES) * LANES
    vmem = pl.BlockSpec(memory_space=pltpu.VMEM)
    smem = pl.BlockSpec(memory_space=pltpu.SMEM)
    hbm = pl.BlockSpec(memory_space=pl.ANY)
    dma = pltpu.SemaphoreType.DMA

    def by_head(reps_of):
        return jnp.transpose(reps_of, (1, 0, 2, 3)).reshape(kv_heads, reps, width)

    partial, lse = pl.pallas_call(
        attend_kernel,
        out_shape=(
            jax.ShapeDtypeStruct((shares, rows, width), jnp.bfloat16),
            jax.ShapeDtypeStruct((shares, 8, LANES), jnp.float32),
        ),
        in_specs=[smem, vmem, vmem, vmem, vmem, hbm, hbm],
        out_specs=(vmem, vmem),
        scratch_shapes=[
            pltpu.VMEM((kv_heads, blocks, span, width), jnp.bfloat16),
            pltpu.VMEM((kv_heads, blocks, span, width), jnp.bfloat16),
            pltpu.VMEM((8, lanes), jnp.int32),
            pltpu.SMEM((8, lanes), jnp.int32),
            pltpu.VMEM((kv_heads, tokens * group, width), jnp.bfloat16),
            pltpu.VMEM((kv_heads, tokens * group, reps), jnp.float32),
            pltpu.VMEM((capacity, group, span), jnp.float32),
            pltpu.VMEM((kv_heads, tokens, group, LANES), jnp.float32),
            pltpu.VMEM((kv_heads, tokens, group, LANES), jnp.float32),
            pltpu.VMEM((kv_heads, tokens, group, width), jnp.float32),
            dma((kv_heads, PIECES)),
            dma((kv_heads, PIECES)),
            dma,
        ],
        compiler_params=pltpu.CompilerParams(vmem_limit_bytes=40 * 1024 * 1024),
    )(block_counts, block_ids, queries, by_head(rep_keys), by_head(rep_values), keys, values)

    return pl.pallas_call(
        functools.partial(finish_kernel, shares, groups),
        out_shape=jax.ShapeDtypeStruct((tokens // groups, columns), jnp.bfloat16),
        in_specs=[vmem, vmem, hbm],
        out_specs=vmem,
        scratch_shapes=[
            pltpu.VMEM(out_weight.shape, jnp.bfloat16),
            pltpu.VMEM((shares, rows, width), jnp.bfloat16),
            pltpu.VMEM((shares, 8, LANES), jnp.float32),
            pltpu.VMEM((shares, rows, width), jnp.bfloat16),
            pltpu.VMEM((tokens, columns), jnp.float32),
            pltpu.VMEM((groups, tokens // groups, columns), jnp.bfloat16),
            pltpu.VMEM((groups, tokens // groups, columns), jnp.bfloat16),
            dma((shares,)),
            dma((shares,)),
            dma((shares,)),
            dma((shares,)),
            dma((shares,)),
            dma((shares,)),
            dma((shares,)),
            dma((groups,)),
            dma((groups,)),
        ],
        compiler_params=pltpu.CompilerParams(
            collective_id=0, has_side_effects=True, vmem_limit_bytes=20 * 1024 * 1024
        ),
    )(partial, lse, out_weight)


def solution(mesh):
    in_specs = (
        P(None, "kvh", None),
        P("seq", "kvh", None, None),
        P("seq", "kvh", None, None),
        P("seq", "kvh", None, None),
        P("seq", "kvh", None, None),
        P(None, "kvh", None),
        P("seq"),
        P("kvh", "seq"),
    )
    return jax.shard_map(
        functools.partial(on_device, mesh.shape["seq"], mesh.shape["kvh"]),
        mesh=mesh, in_specs=in_specs, out_specs=P("kvh", "seq"), check_vma=False,
    )
```

time: 205 us -> 48.6 us (0.24)
  waiting for transfers between devices: 54.9 us -> 0 us
  local copies, waits for them, and re-layouts: 60 us -> 8.5 us
  Pallas kernels: 0 us -> 39.8 us
  matrix products: 37.7 us -> 0 us
  blocking collectives: 20.6 us -> 0 us
  other arithmetic: 17 us -> 0 us
  between operations: 13.4 us -> 0.04 us
    gather x6 -> x0, local copies, waits for them, and re-layouts: 47.5 us -> none  [the longest x1 19.8 us: on_device(): tile_vals = values[slot_block, head_pos[:, None]]]
    pallas_call x0 -> x2, Pallas kernels: none -> 39.8 us  [the longest x1 23.5 us: on_device(): pl.pallas_call(functools.partial(finish_kernel, shares, groups), out_shap...]
    dot_general x7 -> x0, matrix products: 37.7 us -> none  [the longest x1 9.76 us: summary_stats(): jnp.einsum('bkgd,nkrd->bkgrn', query_rows, summary_keys, preferred_elemen...]
    all_gather x3 -> x0, waiting for transfers between devices: 35.1 us -> none  [the longest x1 28.4 us: on_device(): lax.all_gather(rep_keys, 'seq', axis=0, tiled=True)]
    all_gather x2 -> x0, blocking collectives: 20.6 us -> none  [joined(): lax.all_gather(part.astype(kind), axis)]
    reduce_scatter x1 -> x0, waiting for transfers between devices: 19.7 us -> none  [on_device(): lax.psum_scatter(terms.astype(jnp.bfloat16), 'kvh', scatter_dimension=0,...]
    reduce_sum x3 -> x0, other arithmetic: 10.3 us -> none  [the longest x1 8.64 us: summary_stats(): weight_sum = jnp.sum(weights, axis=(3, 4))]
    dynamic_slice x7 -> x0, local copies, waits for them, and re-layouts: 6.88 us -> none  [take(): part[k].astype(own.dtype)]
  transfers between devices with their start and end apart: 4 -> 0, of which waited for: 3 -> 0; matrix products, arithmetic and copies ran while one was open for 17% -> 0% of each run, Pallas kernels for 0% -> 0%
where the time goes in v1:
time: 48.6 us; the launch traced here: 48.4 us
  Pallas kernels  39.8 us (82%)
  local copies, waits for them, and re-layouts  8.5 us (17%)
    pallas_call x1, Pallas kernels, on_device(): pl.pallas_call(functools.partial(finish_kernel, shares, groups), out_shap...  23.5 us
    pallas_call x1, Pallas kernels, on_device(): pl.pallas_call(attend_kernel, out_shape=(jax.ShapeDtypeStruct((shares, ro...  16.3 us
    unnamed x10, local copies, waits for them, and re-layouts  6.41 us
    transpose x2, local copies, waits for them, and re-layouts, by_head(): return jnp.transpose(reps_of, (1, 0, 2, 3)).reshape(kv_heads, reps, width)  2.09 us

profile of v1, /device:TPU:0, one launch (start us, length us, event | category | flops | bytes accessed | tf_op | source)
XLA Modules:
  0.0 48.4 jit_solution(14581958237302002724)
XLA Ops:
  0.0 0.8 %copy.11.ids_ref = s32[64,2,16]{2,1,0:T(2,128)S(1)} copy(s32[64,2,16]{0,2,1:T(8,128)} %param.13) | data formatting | bytes 16384 | tf_op args[5]
  0.8 1.0 %copy.9 = bf16[2,128,4,128]{3,2,1,0:T(4,128)(2,1)S(1)} copy(bf16[2,128,4,128]{3,2,0,1:T(4,128)(2,1)} %bitcast.6) | data formatting | bytes 524288 | tf_op jit(solution)/shard_map/transpose | solution.py:296
  1.9 1.0 %copy.10 = bf16[2,128,4,128]{3,2,1,0:T(4,128)(2,1)S(1)} copy(bf16[2,128,4,128]{3,2,0,1:T(4,128)(2,1)} %bitcast.7) | data formatting | bytes 524288 | tf_op jit(solution)/shard_map/transpose | solution.py:296
  2.9 0.0 copy-start
  2.9 3.4 %copy-done = bf16[128,2,128,128]{3,2,1,0:T(8,128)(2,1)S(1)} copy-done((bf16[128,2,128,128]{3,2,1,0:T(8,128)(2,1)S(1)}, bf16[128,2,128,128]{3,2,1,0:T(8,128)(2,1)}, u32[]{:S(2)}) %copy-start) | copy-done | bytes 8388632
  6.3 0.0 copy-start.2
  6.3 0.9 %copy-done.2 = bf16[64,16,128]{2,1,0:T(8,128)(2,1)S(1)} copy-done((bf16[64,16,128]{2,1,0:T(8,128)(2,1)S(1)}, bf16[64,16,128]{2,1,0:T(8,128)(2,1)}, u32[]{:S(2)}) %copy-start.2) | copy-done | bytes 262168
  7.2 0.0 copy-start.3
  7.2 0.7 %copy-done.3 = s32[128]{0:T(128)S(1)} copy-done((s32[128]{0:T(128)S(1)}, s32[128]{0:T(128)}, u32[]{:S(2)}) %copy-start.3) | copy-done | bytes 536
  7.9 0.0 copy-start.1
  7.9 16.3 %shard_map.82 = (bf16[8,128,128]{2,1,0:T(8,128)(2,1)S(1)}, f32[8,8,128]{2,1,0:T(8,128)S(1)}) custom-call(s32[128]{0:T(128)S(1)} %copy-done.3, s32[64,2,16]{2,1,0:T(2,128)S(1)} %copy.11.ids_ref, bf16[64,16,128]{2,1,0:T(8,128)(2,1)S(1)} %copy-done.2, bf16[2,512,128]{2,1,0:T(8,128)(2,1)S(1)} %bitcast.4, bf16[2,512,128]{2,1,0:T(8,128)(2,1)S(1)} %bitcast.5, ...), custom_call_target="tpu_custom_call" | custom-call | tf_op jit(solution)/shard_map/pallas_call | solution.py:298
  24.2 0.0 copy-done.1
  24.2 23.5 %shard_map.83 = bf16[16,1024]{1,0:T(8,128)(2,1)S(1)} custom-call(bf16[8,128,128]{2,1,0:T(8,128)(2,1)S(1)} %get-tuple-element.7.o_ref, f32[8,8,128]{2,1,0:T(8,128)S(1)} %get-tuple-element.8.lse_ref, bf16[2048,1024]{1,0:T(8,128)(2,1)S(1)} %copy-done.1), custom_call_target="tpu_custom_call" | custom-call | tf_op jit(solution)/shard_map/pallas_call | solution.py:324
  47.7 0.6 %copy.13 = bf16[16,1024]{1,0:T(8,128)(2,1)} copy(bf16[16,1024]{1,0:T(8,128)(2,1)S(1)} %shard_map.83) | data formatting | bytes 65536
Async XLA Ops:
  2.9 3.4 %copy-start = (bf16[128,2,128,128]{3,2,1,0:T(8,128)(2,1)S(1)}, bf16[128,2,128,128]{3,2,1,0:T(8,128)(2,1)}, u32[]{:S(2)}) copy-start(bf16[128,2,128,128]{3,2,1,0:T(8,128)(2,1)} %keys_ref.1) | copy-start | bytes 25165828
  6.3 0.9 %copy-start.2 = (bf16[64,16,128]{2,1,0:T(8,128)(2,1)S(1)}, bf16[64,16,128]{2,1,0:T(8,128)(2,1)}, u32[]{:S(2)}) copy-start(bf16[64,16,128]{2,1,0:T(8,128)(2,1)} %q_ref.1) | copy-start | bytes 786436
  7.2 0.7 %copy-start.3 = (s32[128]{0:T(128)S(1)}, s32[128]{0:T(128)}, u32[]{:S(2)}) copy-start(s32[128]{0:T(128)} %counts_ref.1) | copy-start | bytes 1540
  7.9 16.3 %copy-start.1 = (bf16[2048,1024]{1,0:T(8,128)(2,1)S(1)}, bf16[2048,1024]{1,0:T(8,128)(2,1)}, u32[]{:S(2)}) copy-start(bf16[2048,1024]{1,0:T(8,128)(2,1)} %w_ref.1) | copy-start | bytes 12582916

commit v2 on v1

--- a/solution.py
+++ b/solution.py
@@ -24,14 +24,15 @@
 
 
 def attend_kernel(
-    counts_ref, ids_ref, q_ref, rk_ref, rv_ref, keys_ref, values_ref, o_ref, lse_ref,
-    k_mem, v_mem, slots_v, slots_s, qh, sums, sc, top, low, acc, k_sem, v_sem, slot_sem,
+    counts_hbm, ids_hbm, q_hbm, rk_hbm, rv_hbm, keys_ref, values_ref, o_ref, lse_ref,
+    counts_ref, ids_ref, q_ref, rk_mem, rv_mem,
+    k_mem, v_mem, slots_v, slots_s, qh, sums, sc, top, low, acc, k_sem, v_sem, slot_sem, in_sem,
 ):
     tokens, heads, width = q_ref.shape
     kv_heads, blocks, span, _ = k_mem.shape
     group = heads // kv_heads
-    reps = rk_ref.shape[1]
-    chosen = ids_ref.shape[2]
+    reps = blocks * rk_mem.shape[2]
+    chosen = ids_ref.shape[1]
     lanes = slots_v.shape[1]
     inv_root = 1.0 / math.sqrt(width)
     me = lax.axis_index("seq")
@@ -42,6 +43,19 @@
         rows = pl.ds(i * part, part)
         return pltpu.make_async_copy(source.at[rows, k], target.at[k, rows], sem.at[k, i])
 
+    ids_copy = pltpu.make_async_copy(ids_hbm, ids_ref, in_sem.at[0])
+    counts_copy = pltpu.make_async_copy(counts_hbm, counts_ref, in_sem.at[1])
+    q_copy = pltpu.make_async_copy(q_hbm, q_ref, in_sem.at[2])
+    rk_copies = [
+        pltpu.make_async_copy(rk_hbm.at[:, k], rk_mem.at[k], in_sem.at[3 + k])
+        for k in range(kv_heads)
+    ]
+    rv_copies = [
+        pltpu.make_async_copy(rv_hbm.at[:, k], rv_mem.at[k], in_sem.at[3 + kv_heads + k])
+        for k in range(kv_heads)
+    ]
+    for copy in [ids_copy, counts_copy, q_copy] + rk_copies + rv_copies:
+        copy.start()
     for k in range(kv_heads):
         for i in range(PIECES):
             copy_of(k, i, keys_ref, k_mem, k_sem).start()
@@ -58,16 +72,23 @@
         lax.broadcasted_iota(jnp.int32, (tokens, tokens), 1)
         < lax.broadcasted_iota(jnp.int32, (tokens, tokens), 0)
     ).astype(jnp.bfloat16)
+    same_token = (
+        lax.broadcasted_iota(jnp.int32, (tokens, tokens), 1)
+        == lax.broadcasted_iota(jnp.int32, (tokens, tokens), 0)
+    ).astype(jnp.bfloat16)
     every_slot = jnp.ones((chosen, chosen), jnp.bfloat16)
     slots_v[...] = jnp.zeros_like(slots_v)
+    ids_copy.wait()
     for k in range(kv_heads):
-        ids = ids_ref[:, k, :] - me * blocks
-        here = (ids >= 0) & (ids < blocks)
+        ids = ids_ref[k] - me * blocks
+        ids = jnp.where((ids >= 0) & (ids < blocks), ids + 1, 0).astype(jnp.float32)
+        place = contract_last(same_token, ids.astype(jnp.bfloat16)).astype(jnp.int32)
+        here = place > 0
         mark = jnp.where(here, 1.0, 0.0).astype(jnp.bfloat16)
         of_token = matmul(mark, every_slot)
         rank = matmul(mark, before_slot) + matmul(before_token, of_token.astype(jnp.bfloat16))
         rank = jnp.where(here, rank.astype(jnp.int32), -1)
-        code = token_of * blocks + ids + 1
+        code = token_of * blocks + place
         found = jnp.zeros((tokens, lanes), jnp.int32)
         for s in range(chosen):
             found = found + jnp.where(rank[:, s : s + 1] == slot_of, code[:, s : s + 1], 0)
@@ -77,17 +98,20 @@
     slot_copy = pltpu.make_async_copy(slots_v, slots_s, slot_sem)
     slot_copy.start()
 
+    for copy in [q_copy] + rk_copies:
+        copy.wait()
     for k in range(kv_heads):
         mine = q_ref[...].astype(jnp.float32)[:, k * group : (k + 1) * group, :]
         qh[k] = mine.reshape(tokens * group, width).astype(jnp.bfloat16)
-        scores = contract_last(qh[k], rk_ref[k]) * inv_root
+        scores = contract_last(qh[k], rk_mem[k].reshape(reps, width)) * inv_root
         sums[k] = scores
         most = scores[:, :LANES]
         for c in range(LANES, reps, LANES):
             most = jnp.maximum(most, scores[:, c : c + LANES])
         top[k] = most.reshape(tokens, group, LANES)
 
-    slot_copy.wait()
+    for copy in [slot_copy, counts_copy] + rv_copies:
+        copy.wait()
     lane = lax.broadcasted_iota(jnp.int32, (group, span), 1)
 
     def slot(k, j):
@@ -127,7 +151,7 @@
         for c in range(LANES, reps, LANES):
             some = some + weights[:, c : c + LANES]
         low[k] = some.reshape(tokens, group, LANES)
-        acc[k] = matmul(weights.astype(jnp.bfloat16), rv_ref[k]).reshape(tokens, group, width)
+        acc[k] = matmul(weights.astype(jnp.bfloat16), rv_mem[k].reshape(reps, width)).reshape(tokens, group, width)
 
         for i in range(PIECES):
             copy_of(k, i, values_ref, v_mem, v_sem).wait()
@@ -288,12 +312,9 @@
     capacity = -(-3 * tokens // UNROLL) * UNROLL
     lanes = -(-capacity // LANES) * LANES
     vmem = pl.BlockSpec(memory_space=pltpu.VMEM)
-    smem = pl.BlockSpec(memory_space=pltpu.SMEM)
-    hbm = pl.BlockSpec(memory_space=pl.ANY)
+    by_slot = jnp.transpose(block_ids, (1, 2, 0))
+    hbm = pl.BlockSpec(memory_space=pltpu.HBM)
     dma = pltpu.SemaphoreType.DMA
-
-    def by_head(reps_of):
-        return jnp.transpose(reps_of, (1, 0, 2, 3)).reshape(kv_heads, reps, width)
 
     partial, lse = pl.pallas_call(
         attend_kernel,
@@ -301,9 +322,14 @@
             jax.ShapeDtypeStruct((shares, rows, width), jnp.bfloat16),
             jax.ShapeDtypeStruct((shares, 8, LANES), jnp.float32),
         ),
-        in_specs=[smem, vmem, vmem, vmem, vmem, hbm, hbm],
+        in_specs=[hbm] * 7,
         out_specs=(vmem, vmem),
         scratch_shapes=[
+            pltpu.SMEM(block_counts.shape, jnp.int32),
+            pltpu.VMEM(by_slot.shape, jnp.int32),
+            pltpu.VMEM(queries.shape, jnp.bfloat16),
+            pltpu.VMEM((kv_heads, blocks) + rep_keys.shape[2:], jnp.bfloat16),
+            pltpu.VMEM((kv_heads, blocks) + rep_keys.shape[2:], jnp.bfloat16),
             pltpu.VMEM((kv_heads, blocks, span, width), jnp.bfloat16),
             pltpu.VMEM((kv_heads, blocks, span, width), jnp.bfloat16),
             pltpu.VMEM((8, lanes), jnp.int32),
@@ -317,9 +343,10 @@
             dma((kv_heads, PIECES)),
             dma((kv_heads, PIECES)),
             dma,
+            dma((3 + 2 * kv_heads,)),
         ],
-        compiler_params=pltpu.CompilerParams(vmem_limit_bytes=40 * 1024 * 1024),
-    )(block_counts, block_ids, queries, by_head(rep_keys), by_head(rep_values), keys, values)
+        compiler_params=pltpu.CompilerParams(vmem_limit_bytes=67043328),
+    )(block_counts, by_slot, queries, rep_keys, rep_values, keys, values)
 
     return pl.pallas_call(
         functools.partial(finish_kernel, shares, groups),
@@ -345,7 +372,7 @@
             dma((groups,)),
         ],
         compiler_params=pltpu.CompilerParams(
-            collective_id=0, has_side_effects=True, vmem_limit_bytes=20 * 1024 * 1024
+            collective_id=0, has_side_effects=True, vmem_limit_bytes=60 * 1024 * 1024
         ),
     )(partial, lse, out_weight)
 

time: 48.6 us -> 45.9 us (0.944)
  local copies, waits for them, and re-layouts: 8.5 us -> 1.38 us
  Pallas kernels: 39.8 us -> 44.3 us
    unnamed x10 -> x1, local copies, waits for them, and re-layouts: 6.41 us -> 1.38 us
    pallas_call x1, Pallas kernels: 16.3 us -> 19 us  [on_device(): pl.pallas_call(attend_kernel, out_shape=(jax.ShapeDtypeStruct((shares, ro...]
    transpose x2 -> x0, local copies, waits for them, and re-layouts: 2.09 us -> none  [by_head(): return jnp.transpose(reps_of, (1, 0, 2, 3)).reshape(kv_heads, reps, width)]
    pallas_call x1, Pallas kernels: 23.5 us -> 25.2 us  [on_device(): pl.pallas_call(functools.partial(finish_kernel, shares, groups), out_shap...]
where the time goes in v2:
time: 45.9 us; the launch traced here: 45.7 us
  Pallas kernels  44.3 us (97%)
  local copies, waits for them, and re-layouts  1.38 us (3%)
    pallas_call x1, Pallas kernels, on_device(): pl.pallas_call(functools.partial(finish_kernel, shares, groups), out_shap...  25.2 us
    pallas_call x1, Pallas kernels, on_device(): pl.pallas_call(attend_kernel, out_shape=(jax.ShapeDtypeStruct((shares, ro...  19 us
    unnamed x1, local copies, waits for them, and re-layouts  1.38 us

profile of v2, /device:TPU:0, one launch (start us, length us, event | category | flops | bytes accessed | tf_op | source)
XLA Modules:
  0.0 45.7 jit_solution(2024539365757024813)
XLA Ops:
  0.0 19.0 %shard_map.82 = (bf16[8,128,128]{2,1,0:T(8,128)(2,1)}, f32[8,8,128]{2,1,0:T(8,128)}) custom-call(s32[128]{0:T(128)} %counts_hbm.1, s32[2,16,64]{2,1,0:T(8,128)} %bitcast.1, bf16[64,16,128]{2,1,0:T(8,128)(2,1)} %q_hbm.1, bf16[128,2,4,128]{3,2,1,0:T(4,128)(2,1)} %rk_hbm.1, bf16[128,2,4,128]{3,2,1,0:T(4,128)(2,1)} %rv_hbm.1, ...), custom_call_target="tpu_custom_call" | custom-call | tf_op jit(solution)/shard_map/pallas_call | solution.py:319
  19.1 25.2 %shard_map.83 = bf16[16,1024]{1,0:T(8,128)(2,1)} custom-call(bf16[8,128,128]{2,1,0:T(8,128)(2,1)} %get-tuple-element.7.o_ref, f32[8,8,128]{2,1,0:T(8,128)} %get-tuple-element.8.lse_ref, bf16[2048,1024]{1,0:T(8,128)(2,1)} %w_ref.1), custom_call_target="tpu_custom_call" | custom-call | tf_op jit(solution)/shard_map/pallas_call | solution.py:351
  44.3 1.4 %copy.10 = bf16[16,1024]{1,0:T(8,128)(2,1)} copy(bf16[16,1024]{1,0:T(8,128)(2,1)} %shard_map.83) | data formatting | bytes 65536
